TPU v7x, 32 devices: a whole 2x2x4 slice. The times are simulated.
32 devices in a mesh: rep: 2 (over y), tp: 4 (over z), ep: 4 (over x, core).
Axes of the slice: x: 2, y: 2, z: 4, core: 2. Of those that a mesh axis runs over, the one named last changes fastest.
Arguments:
- tokens: bfloat16 [768, 3072], P(('rep', 'ep'), 'tp'), parts along dimension 0, may hold values from -6 to 6
- routing: int32 [768, 2], P(('rep', 'ep')), parts along dimension 0, may hold values from 0 to 3, all different within a row; in each aligned block of 96 rows (0 to 95, 96 to 191, ...) at most 54 rows name the same one
- route_gates: float32 [768, 2], P(('rep', 'ep')), parts along dimension 0, may hold values from 0.2 to 1
- expert_gate: bfloat16 [4, 3072, 8192], P('ep', None, 'tp'), may hold values from -0.109375 to 0.109375
- expert_up: bfloat16 [4, 3072, 8192], P('ep', None, 'tp'), may hold values from -0.109375 to 0.109375
- expert_down: bfloat16 [4, 8192, 3072], P('ep', 'tp'), may hold values from -0.0625 to 0.0625
Outputs:
- mixture: bfloat16 [768, 3072], P(('rep', 'ep'), 'tp'), parts along dimension 0
There are 2 independent parts, one for each index of `rep`. A program takes and returns all parts, laid end to end along the dimension named above; an argument that names none is the same for every part. Nothing has to cross between parts.
Inputs may be any that keep to these rules, and one draw needn't show every extreme that they name: `routing`: each token names two different experts. In each aligned block of 96 tokens (the rows of one index of ep) no expert is named by more than 54 tokens, a bound that some block reaches.
All inputs are finite; a program needn't handle non-finite values.
Results may differ from a plain program's by a relative error of at most 0.0085.
Values may be sent and summed in bfloat16 or wider, within the bound.
A program may use at most 128 MiB of HBM per device.

v0:
```python
import functools

import jax
import jax.numpy as jnp
from jax import lax
from jax.experimental import pallas as pl
from jax.experimental.pallas import tpu as pltpu
from jax.sharding import PartitionSpec as P


def slot_tables(routing, route_gates, experts, capacity):
    count_rows = routing.shape[0]
    choices_n = routing.shape[1]
    flat_ids = routing.reshape(-1)
    onehot = (flat_ids[:, None] == jnp.arange(experts, dtype=jnp.int32)[None, :]).astype(jnp.int32)
    before = jnp.cumsum(onehot, axis=0) - onehot
    position = jnp.sum(before * onehot, axis=1)
    slot_index = flat_ids * capacity + position
    picked = (
        slot_index[:, None] == jnp.arange(experts * capacity, dtype=jnp.int32)[None, :]
    ).astype(jnp.float32)
    dispatch = picked.reshape(count_rows, choices_n, experts * capacity).sum(axis=1)
    combine = (
        (picked * route_gates.reshape(-1)[:, None])
        .reshape(count_rows, choices_n, experts * capacity)
        .sum(axis=1)
    )
    return (dispatch, combine)


def hidden_rows(everyone, expert_gate, expert_up, capacity):
    local_count = expert_gate.shape[0]
    total = everyone.shape[0]
    row_block = everyone.reshape(
        total // (local_count * capacity), local_count, capacity, everyone.shape[1]
    )
    gate_part = jnp.einsum(
        "tlcd,ldf->tlcf", row_block, expert_gate, preferred_element_type=jnp.float32
    )
    upward = jnp.einsum("tlcd,ldf->tlcf", row_block, expert_up, preferred_element_type=jnp.float32)
    return (jax.nn.silu(gate_part) * upward).astype(jnp.bfloat16)


def plain_body(tokens, routing, route_gates, expert_gate, expert_up, expert_down):
    local_count = expert_gate.shape[0]
    ep_count = lax.axis_size("ep")
    tp_count = lax.axis_size("tp")
    tok_count = tokens.shape[0]
    capacity = 2 * tok_count // ep_count + tok_count // 16
    experts = local_count * ep_count
    dispatch, combine = slot_tables(routing, route_gates, experts, capacity)
    dispatch_low = dispatch.astype(jnp.bfloat16)
    whole = lax.all_gather(tokens, "tp", axis=1, tiled=True)
    packed = jnp.einsum(
        "tc,td->cd", dispatch_low, whole, preferred_element_type=jnp.float32
    ).astype(jnp.bfloat16)
    everyone = lax.all_to_all(packed, "ep", split_axis=0, concat_axis=0, tiled=True)
    total_rows = everyone.shape[0]
    columns = everyone.shape[1]
    hidden = hidden_rows(everyone, expert_gate, expert_up, capacity)
    part = jnp.einsum("tlcf,lfd->dtlc", hidden, expert_down, preferred_element_type=jnp.float32)
    summed_t = lax.psum_scatter(
        part.reshape(columns // tp_count * lax.axis_size("tp"), total_rows),
        "tp",
        scatter_dimension=0,
        tiled=True,
    )
    summed = summed_t.T
    expert_out = summed.astype(jnp.bfloat16)
    returned = lax.all_to_all(expert_out, "ep", split_axis=0, concat_axis=0, tiled=True)
    mixed = jnp.dot(combine, returned.astype(jnp.float32), precision=lax.Precision.HIGHEST)
    return mixed.astype(jnp.bfloat16)


MESH = pl.DeviceIdType.MESH
LANES = 128


def up_to(value, step):
    return -(-value // step) * step


def rcopy(src, dst, send, recv, device):
    return pltpu.make_async_remote_copy(
        src_ref=src, dst_ref=dst, send_sem=send, recv_sem=recv, device_id=device, device_id_type=MESH
    )


def layer_kernel(
    tp, ep, cap, rows, tokens, meta, gate_hbm, up_hbm, down_hbm, out,
    x, m, pick, place, scale, wg, wu, wd, acc_g, acc_u, packed, hidden, part,
    c, c_in, x_out, x_in, z_out, z_in,
    w_sem, zs, zr, xs, xr, cs, cr, ms, mr, rcs, rcr, rxs, rxr, rzs, rzr,
):
    t = lax.axis_index("tp")
    e = lax.axis_index("ep")
    half = ep // 2
    core = lax.rem(e, 2)
    column = e // 2
    e_core = e + 1 - 2 * core
    e_x = lax.rem(e + half, ep)
    e_xc = lax.rem(e_core + half, ep)
    tok, feat = tokens.shape
    ff = wg.shape[2]
    f32, b16 = jnp.float32, jnp.bfloat16

    def quarter(d):
        return lax.rem(t + tp - d, tp)

    def select(values):
        found = jnp.int32(values[0])
        for k in range(1, tp):
            found = jnp.where(t == k, jnp.int32(values[k]), found)
        return found

    nearest = [sorted(range(tp), key=lambda q, k=k: (abs(q - k), q)) for k in range(tp)]
    arrivals = [select([nearest[k][i] for k in range(tp)]) for i in range(tp)]
    pieces = 2 if tok % 32 == 0 else 1
    piece = tok // pieces

    loads = []
    for d in range(tp):
        q = arrivals[d]
        for k, (src, dst) in enumerate(((gate_hbm, wg), (up_hbm, wu))):
            r = pl.ds(pl.multiple_of(q * feat, feat), feat)
            loads.append(pltpu.make_async_copy(src.at[0, r, :], dst.at[q], w_sem.at[k * tp + d]))
    down_loads = []
    for i in range(tp):
        q = quarter(tp - 1 - i)
        r = pl.ds(pl.multiple_of(q * feat, feat), feat)
        down_loads.append(pltpu.make_async_copy(down_hbm.at[0, :, r], wd.at[q], w_sem.at[2 * tp + i]))
    for load in loads + down_loads:
        load.start()

    pad = x.shape[2] - tok
    for q in range(tp):
        for b in range(ep):
            x[q, b, tok:, :] = jnp.zeros((pad, feat), b16)
    x[t, e, 0:tok, :] = tokens[...]
    m[e] = meta[...]
    part[rows:, :] = jnp.zeros((part.shape[0] - rows, feat), b16)

    barrier = pltpu.get_barrier_semaphore()
    for d in range(1, tp):
        pl.semaphore_signal(barrier, inc=1, device_id={"tp": lax.rem(t + d, tp)}, device_id_type=MESH)
    pl.semaphore_signal(barrier, inc=1, device_id={"ep": e_x}, device_id_type=MESH)
    pl.semaphore_signal(barrier, inc=1, device_id={"ep": e_core}, device_id_type=MESH)
    pl.semaphore_wait(barrier, tp + 1)

    sent = []

    def send(src, dst, s, r, device):
        copy = rcopy(src, dst, s, r, device)
        copy.start()
        sent.append(copy)

    def block(q, b, p):
        return x.at[q, b, pl.ds(p * piece, piece), :]

    some = []

    def send_if(cond, src, dst, s, r, device):
        copy = rcopy(src, dst, s, r, device)
        some.append((cond, copy))

        @pl.when(cond)
        def _():
            copy.start()

    to_x, to_core = {"ep": e_x}, {"ep": e_core}
    send(meta, m.at[e], ms.at[0], mr.at[0], to_x)
    send(meta, m.at[e], ms.at[1], mr.at[1], to_core)
    above, below = {"tp": lax.rem(t + 1, tp)}, {"tp": lax.rem(t + tp - 1, tp)}
    for p in range(pieces):
        own = tokens.at[pl.ds(p * piece, piece), :]
        n = pieces * t + p
        send_if(t < tp - 1, own, block(t, e, p), zs.at[n], zr.at[n], above)
        send_if(t > 0, own, block(t, e, p), zs.at[pieces * tp + n], zr.at[n], below)
        send(own, block(t, e, p), xs.at[n], xr.at[n], to_x)
        send(own, block(t, e, p), cs.at[n], cr.at[n], to_core)

    def got(dst, s, r, device):
        rcopy(dst, dst, s, r, device).wait_recv()

    def take_z(i):
        q = arrivals[i]
        for p in range(pieces):
            n = pieces * q + p
            one = block(q, e, p)
            got(one, zs.at[n], zr.at[n], above)
            send_if((q < t) & (t < tp - 1), one, one, zs.at[n], zr.at[n], above)
            send_if((q > t) & (t > 0), one, one, zs.at[pieces * tp + n], zr.at[n], below)
            send(one, one, xs.at[n], xr.at[n], to_x)
            send(one, one, cs.at[n], cr.at[n], to_core)

    def take_x(i):
        for p in range(pieces):
            n = pieces * arrivals[i] + p
            far = pieces * tp + n
            one = block(arrivals[i], e_x, p)
            got(one, xs.at[n], xr.at[n], to_x)
            send(one, one, cs.at[far], cr.at[far], to_core)

    def take_core(i):
        for p in range(pieces):
            n = pieces * arrivals[i] + p
            far = pieces * tp + n
            got(block(arrivals[i], e_core, p), cs.at[n], cr.at[n], to_core)
            got(block(arrivals[i], e_xc, p), cs.at[far], cr.at[far], to_core)

    got(m.at[e_x], ms.at[0], mr.at[0], to_x)
    send(m.at[e_x], m.at[e_x], ms.at[2], mr.at[2], to_core)
    got(m.at[e_core], ms.at[1], mr.at[1], to_core)
    got(m.at[e_xc], ms.at[2], mr.at[2], to_core)

    slots = pick.shape[0]
    mine = e.astype(f32)
    earlier = (
        lax.broadcasted_iota(jnp.int32, (LANES, LANES), 0)
        < lax.broadcasted_iota(jnp.int32, (LANES, LANES), 1)
    ).astype(b16)
    slot = lax.broadcasted_iota(jnp.int32, (slots, LANES), 0).astype(f32)
    total = jnp.zeros((slots, 1), f32)
    for b in range(ep):
        first, second = m[b, 0:1, :] == mine, m[b, 1:2, :] == mine
        named = jnp.where(first, 1.0, 0.0) + jnp.where(second, 1.0, 0.0)
        weight = jnp.where(first, m[b, 2:3, :], 0.0) + jnp.where(second, m[b, 3:4, :], 0.0)
        spread = jnp.broadcast_to(named, (16, LANES)).astype(b16)
        position = jnp.dot(spread, earlier, preferred_element_type=f32)[0:1, :]
        where_to = jnp.where(named > 0.5, position + float(b * cap), -1.0)
        chosen = jnp.where(slot == where_to, 1.0, 0.0)
        total = total + jnp.sum(chosen * weight, axis=1, keepdims=True)
        pick[:, b * LANES:(b + 1) * LANES] = chosen.astype(b16)
        at = ((b % 2) * half + b // 2) * tok
        place[at:at + tok, :] = chosen.T[0:tok, :].astype(b16)
    scale[...] = jnp.broadcast_to(total, scale.shape)

    step = 512
    tiles = ff // step

    def project(d, last):
        q = arrivals[d]
        loads[2 * d].wait()
        loads[2 * d + 1].wait()
        everyone = x[q].reshape(ep * x.shape[2], feat)
        packed[...] = jnp.dot(pick[0:rows, :], everyone, preferred_element_type=f32).astype(b16)

        def tile(j, carry):
            cols = pl.ds(pl.multiple_of(j * step, step), step)
            g = jnp.dot(packed[...], wg[q, :, cols], preferred_element_type=f32)
            u = jnp.dot(packed[...], wu[q, :, cols], preferred_element_type=f32)
            if d > 0:
                g = g + acc_g[:, cols]
                u = u + acc_u[:, cols]
            if last:
                h = g / (1.0 + jnp.exp(-g)) * u * scale[0:rows, 0:1]
                hidden[:, cols] = h.astype(b16)
            else:
                acc_g[:, cols] = g
                acc_u[:, cols] = u
            return carry

        lax.fori_loop(0, tiles, tile, 0)

    take_x(0)
    for i in range(1, tp - 1):
        take_z(i)
    if tp > 2:
        take_x(1)
    take_core(0)
    project(0, tp == 1)
    take_z(tp - 1)
    for i in range(1, tp):
        if i + 1 < tp:
            take_x(i + 1)
        take_core(i)
        project(i, i == tp - 1)

    width = 256 if feat % 256 == 0 else LANES

    def to_tokens(i):
        q = quarter(tp - 1 - i)
        down_loads[i].wait()

        def tile(j, carry):
            cols = pl.ds(pl.multiple_of(j * width, width), width)
            part[0:rows, cols] = jnp.dot(hidden[...], wd[q, :, cols], preferred_element_type=f32).astype(b16)
            back = jnp.dot(place[...], part[:, cols], preferred_element_type=f32).astype(b16)
            c[i, :, :, cols] = back.reshape(ep, tok, width)
            return carry

        lax.fori_loop(0, feat // width, tile, 0)
        away = pl.ds((1 - core) * half, half)
        send(c.at[i, away], c_in.at[i], rcs.at[i], rcr.at[i], to_core)

    def part_of(p):
        return slice(p * piece, (p + 1) * piece)

    def sum_core(i):
        got(c_in.at[i], rcs.at[i], rcr.at[i], to_core)
        far = 1 - column
        for p in range(pieces):
            r = part_of(p)
            value = c[i, core * half + far, r].astype(f32) + c_in[i, far, r].astype(f32)
            x_out[i, r] = value.astype(b16)
            n = pieces * i + p
            view = pl.ds(p * piece, piece)
            send(x_out.at[i, view], x_in.at[i, view], rxs.at[n], rxr.at[n], to_x)

    def sum_x(i, p):
        r, n = part_of(p), pieces * i + p
        got(x_in.at[i, pl.ds(p * piece, piece)], rxs.at[n], rxr.at[n], to_x)
        value = c[i, core * half + column, r].astype(f32) + c_in[i, column, r].astype(f32)
        return value + x_in[i, r].astype(f32)

    for i in range(tp):
        to_tokens(i)
        if i > 0:
            sum_core(i - 1)
    sum_core(tp - 1)
    for i in range(tp - 1):
        for p in range(pieces):
            z_out[i, part_of(p)] = sum_x(i, p).astype(b16)
            n = pieces * i + p
            view = pl.ds(p * piece, piece)
            peer = {"tp": quarter(tp - 1 - i)}
            send(z_out.at[i, view], z_in.at[i, view], rzs.at[n], rzr.at[n], peer)
    for p in range(pieces):
        result = sum_x(tp - 1, p)
        for i in range(tp - 1):
            n = pieces * i + p
            peer = {"tp": lax.rem(t + tp - 1 - i, tp)}
            got(z_in.at[i, pl.ds(p * piece, piece)], rzs.at[n], rzr.at[n], peer)
            result = result + z_in[i, part_of(p)].astype(f32)
        out[part_of(p), :] = result.astype(b16)
    for cond, copy in some:

        @pl.when(cond)
        def _(copy=copy):
            copy.wait_send()

    for copy in sent:
        copy.wait_send()


def kernel_body(tokens, routing, route_gates, expert_gate, expert_up, expert_down):
    ep, tp = lax.axis_size("ep"), lax.axis_size("tp")
    tok, feat = tokens.shape
    ff = expert_gate.shape[2]
    cap = 2 * tok // ep + tok // 16
    rows = up_to(ep * cap, 16)
    slots = up_to(rows, LANES)
    ids = jnp.pad(routing.astype(jnp.float32).T, ((0, 0), (0, LANES - tok)), constant_values=-1.0)
    weights = jnp.pad(route_gates.T, ((0, 4), (0, LANES - tok)))
    meta = jnp.concatenate([ids, weights], axis=0)
    f32, b16 = jnp.float32, jnp.bfloat16
    dma = pltpu.SemaphoreType.DMA
    vmem = pl.BlockSpec(memory_space=pltpu.VMEM)
    hbm = pl.BlockSpec(memory_space=pl.ANY)
    return pl.pallas_call(
        functools.partial(layer_kernel, tp, ep, cap, rows),
        out_shape=jax.ShapeDtypeStruct((tok, feat), b16),
        in_specs=[vmem, vmem, hbm, hbm, hbm],
        out_specs=vmem,
        scratch_shapes=[
            pltpu.VMEM((tp, ep, LANES, feat), b16),
            pltpu.VMEM((ep, 8, LANES), f32),
            pltpu.VMEM((slots, ep * LANES), b16),
            pltpu.VMEM((ep * tok, slots), b16),
            pltpu.VMEM((slots, LANES), f32),
            pltpu.VMEM((tp, feat, ff), b16),
            pltpu.VMEM((tp, feat, ff), b16),
            pltpu.VMEM((tp, ff, feat), b16),
            pltpu.VMEM((rows, ff), f32),
            pltpu.VMEM((rows, ff), f32),
            pltpu.VMEM((rows, feat), b16),
            pltpu.VMEM((rows, ff), b16),
            pltpu.VMEM((slots, feat), b16),
            pltpu.VMEM((tp, ep, tok, feat), b16),
            pltpu.VMEM((tp, ep // 2, tok, feat), b16),
            pltpu.VMEM((tp, tok, feat), b16),
            pltpu.VMEM((tp, tok, feat), b16),
            pltpu.VMEM((tp, tok, feat), b16),
            pltpu.VMEM((tp, tok, feat), b16),
            dma((3 * tp,)),
            dma((4 * tp,)), dma((2 * tp,)),
            dma((2 * tp,)), dma((2 * tp,)),
            dma((4 * tp,)), dma((4 * tp,)),
            dma((3,)), dma((3,)),
            dma((tp,)), dma((tp,)),
            dma((2 * tp,)), dma((2 * tp,)),
            dma((2 * tp,)), dma((2 * tp,)),
        ],
        compiler_params=pltpu.CompilerParams(
            collective_id=0, has_side_effects=True, vmem_limit_bytes=60 * 1024 * 1024
        ),
    )(tokens, meta, expert_gate, expert_up, expert_down)


def body(tokens, routing, route_gates, expert_gate, expert_up, expert_down):
    ep, tp = lax.axis_size("ep"), lax.axis_size("tp")
    tok, feat = tokens.shape
    ff = expert_gate.shape[2]
    fits = ep == 4 and tp > 2 and expert_gate.shape[0] == 1 and tok <= LANES and tok % 16 == 0
    fits = fits and feat % LANES == 0 and ff % 512 == 0 and 3 * tp * feat * ff * 2 <= 40 << 20
    run = kernel_body if fits else plain_body
    return run(tokens, routing, route_gates, expert_gate, expert_up, expert_down)


def solution(mesh):
    return jax.shard_map(
        body,
        mesh=mesh,
        in_specs=(
            P(("rep", "ep"), "tp"),
            P(("rep", "ep"), None),
            P(("rep", "ep"), None),
            P("ep", None, "tp"),
            P("ep", None, "tp"),
            P("ep", "tp", None),
        ),
        out_specs=P(("rep", "ep"), "tp"),
        check_vma=False,
    )
```

profile of v0, /device:TPU:0, one launch (start us, length us, event | category | flops | bytes accessed | tf_op | source)
XLA Modules:
  0.0 56.5 jit_solution(8677646399630796606)
XLA Ops:
  0.0 0.7 %convert_bitcast_fusion = f32[2,96]{1,0:T(2,128)S(1)} fusion(s32[96,2]{0,1:T(2,128)} %param.7), kind=kLoop, calls=%fused_computation.3 | loop fusion | flops 192 | bytes 1536 | tf_op jit(solution)/shard_map/transpose | solution.py:353
  0.7 1.3 %select_maximum_fusion.meta = f32[8,128]{1,0:T(8,128)} fusion(f32[2,96]{1,0:T(2,128)} %bitcast.3, f32[2,96]{1,0:T(2,128)S(1)} %convert_bitcast_fusion), kind=kLoop, calls=%fused_computation | loop fusion | flops 5120 | bytes 5632 | tf_op jit(solution)/shard_map/concatenate | solution.py:355
  2.0 52.9 %shard_map.64 = bf16[96,768]{1,0:T(8,128)(2,1)} custom-call(bf16[96,768]{1,0:T(8,128)(2,1)} %tokens.1, f32[8,128]{1,0:T(8,128)} %select_maximum_fusion.meta, bf16[1,3072,2048]{2,1,0:T(8,128)(2,1)} %gate_hbm.1, bf16[1,3072,2048]{2,1,0:T(8,128)(2,1)} %up_hbm.1, bf16[1,2048,3072]{2,1,0:T(8,128)(2,1)} %down_hbm.1), custom_call_target="tpu_custom_call" | custom-call | tf_op jit(solution)/shard_map/pallas_call | solution.py:360
  54.9 1.6 %copy.8 = bf16[96,768]{1,0:T(8,128)(2,1)} copy(bf16[96,768]{1,0:T(8,128)(2,1)} %shard_map.64) | data formatting | bytes 294912
where the time goes:
time: 56.7 us; the launch traced here: 56.5 us
  Pallas kernels  52.9 us (93%)
  other arithmetic  1.96 us (3%)
  local copies, waits for them, and re-layouts  1.58 us (3%)
    pallas_call x1, Pallas kernels, kernel_body(): pl.pallas_call(functools.partial(layer_kernel, tp, ep, cap, rows), out_sh...  52.9 us
    unnamed x1, local copies, waits for them, and re-layouts  1.58 us
    concatenate x1, other arithmetic, kernel_body(): meta = jnp.concatenate([ids, weights], axis=0)  1.28 us

commit v1 on v0

--- a/solution.py
+++ b/solution.py
@@ -87,10 +87,10 @@
 
 
 def layer_kernel(
-    tp, ep, cap, rows, tokens, meta, gate_hbm, up_hbm, down_hbm, out,
-    x, m, pick, place, scale, wg, wu, wd, acc_g, acc_u, packed, hidden, part,
+    tp, ep, cap, rows, tokens, routing, gates, gate_hbm, up_hbm, down_hbm, out,
+    x, m, m_own, pick, place, scale, wg, wu, wd, acc_g, acc_u, packed, hidden,
     c, c_in, x_out, x_in, z_out, z_in,
-    w_sem, zs, zr, xs, xr, cs, cr, ms, mr, rcs, rcr, rxs, rxr, rzs, rzr,
+    t_sem, w_sem, zs, zr, xs, xr, cs, cr, ms, mr, rcs, rcr, rxs, rxr, rzs, rzr,
 ):
     t = lax.axis_index("tp")
     e = lax.axis_index("ep")
@@ -103,9 +103,24 @@
     tok, feat = tokens.shape
     ff = wg.shape[2]
     f32, b16 = jnp.float32, jnp.bfloat16
-
-    def quarter(d):
-        return lax.rem(t + tp - d, tp)
+    to_x, to_core = {"ep": e_x}, {"ep": e_core}
+    above, below = {"tp": lax.rem(t + 1, tp)}, {"tp": lax.rem(t + tp - 1, tp)}
+
+    barrier = pltpu.get_barrier_semaphore()
+
+    @pl.when(t < tp - 1)
+    def _():
+        pl.semaphore_signal(barrier, inc=1, device_id=above, device_id_type=MESH)
+
+    @pl.when(t > 0)
+    def _():
+        pl.semaphore_signal(barrier, inc=1, device_id=below, device_id_type=MESH)
+
+    pl.semaphore_signal(barrier, inc=1, device_id=to_x, device_id_type=MESH)
+    pl.semaphore_signal(barrier, inc=1, device_id=to_core, device_id_type=MESH)
+
+    own_load = pltpu.make_async_copy(tokens, x.at[t, e, pl.ds(0, tok), :], t_sem.at[0])
+    own_load.start()
 
     def select(values):
         found = jnp.int32(values[0])
@@ -113,8 +128,14 @@
             found = jnp.where(t == k, jnp.int32(values[k]), found)
         return found
 
-    nearest = [sorted(range(tp), key=lambda q, k=k: (abs(q - k), q)) for k in range(tp)]
-    arrivals = [select([nearest[k][i] for k in range(tp)]) for i in range(tp)]
+    def near(k):
+        return sorted(range(tp), key=lambda q: (abs(q - k), q))
+
+    def far(k):
+        return sorted(range(tp), key=lambda q: (-abs(q - k), abs(2 * q - tp + 1), q))
+
+    arrivals = [select([near(k)[i] for k in range(tp)]) for i in range(tp)]
+    leaving = [select([far(k)[i] for k in range(tp)]) for i in range(tp)]
     pieces = 2 if tok % 32 == 0 else 1
     piece = tok // pieces
 
@@ -126,87 +147,89 @@
             loads.append(pltpu.make_async_copy(src.at[0, r, :], dst.at[q], w_sem.at[k * tp + d]))
     down_loads = []
     for i in range(tp):
-        q = quarter(tp - 1 - i)
+        q = leaving[i]
         r = pl.ds(pl.multiple_of(q * feat, feat), feat)
         down_loads.append(pltpu.make_async_copy(down_hbm.at[0, :, r], wd.at[q], w_sem.at[2 * tp + i]))
-    for load in loads + down_loads:
-        load.start()
-
     pad = x.shape[2] - tok
     for q in range(tp):
         for b in range(ep):
             x[q, b, tok:, :] = jnp.zeros((pad, feat), b16)
-    x[t, e, 0:tok, :] = tokens[...]
-    m[e] = meta[...]
-    part[rows:, :] = jnp.zeros((part.shape[0] - rows, feat), b16)
-
-    barrier = pltpu.get_barrier_semaphore()
-    for d in range(1, tp):
-        pl.semaphore_signal(barrier, inc=1, device_id={"tp": lax.rem(t + d, tp)}, device_id_type=MESH)
-    pl.semaphore_signal(barrier, inc=1, device_id={"ep": e_x}, device_id_type=MESH)
-    pl.semaphore_signal(barrier, inc=1, device_id={"ep": e_core}, device_id_type=MESH)
-    pl.semaphore_wait(barrier, tp + 1)
+    m_own[...] = jnp.full(m_own.shape, -1.0, f32)
+    m_own[0:2, 0:tok] = routing[...].astype(f32)
+    m_own[2:4, 0:tok] = gates[...]
+    m[e] = m_own[...]
+
+    own_load.wait()
+    for load in loads + down_loads:
+        load.start()
+    pl.semaphore_wait(barrier, 2 + jnp.where(t > 0, 1, 0) + jnp.where(t < tp - 1, 1, 0))
 
     sent = []
 
     def send(src, dst, s, r, device):
         copy = rcopy(src, dst, s, r, device)
         copy.start()
-        sent.append(copy)
+        sent.append((None, copy))
 
     def block(q, b, p):
         return x.at[q, b, pl.ds(p * piece, piece), :]
 
-    some = []
-
     def send_if(cond, src, dst, s, r, device):
         copy = rcopy(src, dst, s, r, device)
-        some.append((cond, copy))
+        sent.append((cond, copy))
 
         @pl.when(cond)
         def _():
             copy.start()
 
-    to_x, to_core = {"ep": e_x}, {"ep": e_core}
-    send(meta, m.at[e], ms.at[0], mr.at[0], to_x)
-    send(meta, m.at[e], ms.at[1], mr.at[1], to_core)
-    above, below = {"tp": lax.rem(t + 1, tp)}, {"tp": lax.rem(t + tp - 1, tp)}
     for p in range(pieces):
-        own = tokens.at[pl.ds(p * piece, piece), :]
         n = pieces * t + p
-        send_if(t < tp - 1, own, block(t, e, p), zs.at[n], zr.at[n], above)
-        send_if(t > 0, own, block(t, e, p), zs.at[pieces * tp + n], zr.at[n], below)
-        send(own, block(t, e, p), xs.at[n], xr.at[n], to_x)
-        send(own, block(t, e, p), cs.at[n], cr.at[n], to_core)
+        own = block(t, e, p)
+        send_if(t < tp - 1, own, own, zs.at[n], zr.at[n], above)
+        send_if(t > 0, own, own, zs.at[pieces * tp + n], zr.at[n], below)
+        send(own, own, xs.at[n], xr.at[n], to_x)
+        if p == 0:
+            send(m_own, m.at[e], ms.at[0], mr.at[0], to_x)
+            send(m_own, m.at[e], ms.at[1], mr.at[1], to_core)
+        send(own, own, cs.at[n], cr.at[n], to_core)
 
     def got(dst, s, r, device):
         rcopy(dst, dst, s, r, device).wait_recv()
 
-    def take_z(i):
-        q = arrivals[i]
-        for p in range(pieces):
-            n = pieces * q + p
-            one = block(q, e, p)
-            got(one, zs.at[n], zr.at[n], above)
-            send_if((q < t) & (t < tp - 1), one, one, zs.at[n], zr.at[n], above)
-            send_if((q > t) & (t > 0), one, one, zs.at[pieces * tp + n], zr.at[n], below)
-            send(one, one, xs.at[n], xr.at[n], to_x)
-            send(one, one, cs.at[n], cr.at[n], to_core)
+    def take_z(d, ps):
+        for up in (True, False):
+            q = t - d if up else t + d
+            here = q >= 0 if up else q < tp
+            onward = here & (t < tp - 1) if up else here & (t > 0)
+            away = above if up else below
+            q = jnp.clip(q, 0, tp - 1)
+            for p in ps:
+                n = pieces * q + p
+                one = block(q, e, p)
+                k = n if up else pieces * tp + n
+
+                @pl.when(here)
+                def _(one=one, n=n):
+                    got(one, zs.at[n], zr.at[n], away)
+
+                send_if(onward, one, one, zs.at[k], zr.at[n], away)
+                send_if(here, one, one, xs.at[n], xr.at[n], to_x)
+                send_if(here, one, one, cs.at[n], cr.at[n], to_core)
 
     def take_x(i):
         for p in range(pieces):
             n = pieces * arrivals[i] + p
-            far = pieces * tp + n
+            far_n = pieces * tp + n
             one = block(arrivals[i], e_x, p)
             got(one, xs.at[n], xr.at[n], to_x)
-            send(one, one, cs.at[far], cr.at[far], to_core)
+            send(one, one, cs.at[far_n], cr.at[far_n], to_core)
 
     def take_core(i):
         for p in range(pieces):
             n = pieces * arrivals[i] + p
-            far = pieces * tp + n
+            far_n = pieces * tp + n
             got(block(arrivals[i], e_core, p), cs.at[n], cr.at[n], to_core)
-            got(block(arrivals[i], e_xc, p), cs.at[far], cr.at[far], to_core)
+            got(block(arrivals[i], e_xc, p), cs.at[far_n], cr.at[far_n], to_core)
 
     got(m.at[e_x], ms.at[0], mr.at[0], to_x)
     send(m.at[e_x], m.at[e_x], ms.at[2], mr.at[2], to_core)
@@ -235,7 +258,7 @@
         place[at:at + tok, :] = chosen.T[0:tok, :].astype(b16)
     scale[...] = jnp.broadcast_to(total, scale.shape)
 
-    step = 512
+    step = 1024 if ff % 1024 == 0 else 512
     tiles = ff // step
 
     def project(d, last):
@@ -262,50 +285,66 @@
 
         lax.fori_loop(0, tiles, tile, 0)
 
+    take_z(1, range(pieces))
     take_x(0)
-    for i in range(1, tp - 1):
-        take_z(i)
-    if tp > 2:
-        take_x(1)
     take_core(0)
-    project(0, tp == 1)
-    take_z(tp - 1)
-    for i in range(1, tp):
-        if i + 1 < tp:
-            take_x(i + 1)
+    take_z(2, range(pieces))
+    take_x(1)
+    project(0, False)
+    take_core(1)
+    for d in range(3, tp):
+        take_z(d, range(pieces - 1))
+    project(1, False)
+    for d in range(3, tp):
+        take_z(d, range(pieces - 1, pieces))
+    for i in range(2, tp):
+        take_x(i)
         take_core(i)
         project(i, i == tp - 1)
 
     width = 256 if feat % 256 == 0 else LANES
+    tail = jnp.zeros((slots - rows, width), b16)
+
+    def leaves(i):
+        q = leaving[0]
+        for k in range(1, tp):
+            q = jnp.where(i == k, leaving[k], q)
+        return q
+
+    def down_load(i):
+        r = pl.ds(pl.multiple_of(leaves(i) * feat, feat), feat)
+        return pltpu.make_async_copy(down_hbm.at[0, :, r], wd.at[leaves(i)], w_sem.at[2 * tp + i])
+
+    def to_partner(i):
+        away = pl.ds((1 - core) * half, half)
+        return rcopy(c.at[i, away], c_in.at[i], rcs.at[i], rcr.at[i], to_core)
 
     def to_tokens(i):
-        q = quarter(tp - 1 - i)
-        down_loads[i].wait()
-
-        def tile(j, carry):
-            cols = pl.ds(pl.multiple_of(j * width, width), width)
-            part[0:rows, cols] = jnp.dot(hidden[...], wd[q, :, cols], preferred_element_type=f32).astype(b16)
-            back = jnp.dot(place[...], part[:, cols], preferred_element_type=f32).astype(b16)
+        q = leaves(i)
+        down_load(i).wait()
+        for j in range(feat // width):
+            cols = slice(j * width, (j + 1) * width)
+            part = jnp.dot(hidden[...], wd[q, :, cols], preferred_element_type=f32).astype(b16)
+            part = jnp.concatenate([part, tail], axis=0) if slots > rows else part
+            back = jnp.dot(place[...], part, preferred_element_type=f32).astype(b16)
             c[i, :, :, cols] = back.reshape(ep, tok, width)
-            return carry
-
-        lax.fori_loop(0, feat // width, tile, 0)
-        away = pl.ds((1 - core) * half, half)
-        send(c.at[i, away], c_in.at[i], rcs.at[i], rcr.at[i], to_core)
+        to_partner(i).start()
 
     def part_of(p):
         return slice(p * piece, (p + 1) * piece)
 
+    def to_other_x(i, p):
+        n, view = pieces * i + p, pl.ds(p * piece, piece)
+        return rcopy(x_out.at[i, view], x_in.at[i, view], rxs.at[n], rxr.at[n], to_x)
+
     def sum_core(i):
         got(c_in.at[i], rcs.at[i], rcr.at[i], to_core)
-        far = 1 - column
+        other = 1 - column
         for p in range(pieces):
             r = part_of(p)
-            value = c[i, core * half + far, r].astype(f32) + c_in[i, far, r].astype(f32)
+            value = c[i, core * half + other, r].astype(f32) + c_in[i, other, r].astype(f32)
             x_out[i, r] = value.astype(b16)
-            n = pieces * i + p
-            view = pl.ds(p * piece, piece)
-            send(x_out.at[i, view], x_in.at[i, view], rxs.at[n], rxr.at[n], to_x)
+            to_other_x(i, p).start()
 
     def sum_x(i, p):
         r, n = part_of(p), pieces * i + p
@@ -313,34 +352,68 @@
         value = c[i, core * half + column, r].astype(f32) + c_in[i, column, r].astype(f32)
         return value + x_in[i, r].astype(f32)
 
+    def pass_on(i, p):
+        q = leaving[i]
+        right = q > t
+        view = pl.ds(p * piece, piece)
+        value = sum_x(i, p)
+        behind = (right & (t > 0)) | (~right & (t < tp - 1))
+        n_in = pieces * q + p
+
+        @pl.when(behind)
+        def _():
+            got(z_in.at[q, view], rzs.at[0], rzr.at[n_in], above)
+            z_out[i, part_of(p)] = (value + z_in[q, part_of(p)].astype(f32)).astype(b16)
+
+        @pl.when(~behind)
+        def _():
+            z_out[i, part_of(p)] = value.astype(b16)
+
+        slot_to = jnp.where(~right & (q == t - 1), tp, q)
+        peer = {"tp": jnp.where(right, lax.rem(t + 1, tp), lax.rem(t + tp - 1, tp))}
+        send(
+            z_out.at[i, view], z_in.at[slot_to, view],
+            rzs.at[pieces * i + p], rzr.at[pieces * slot_to + p], peer,
+        )
+
+    to_tokens(0)
+
+    def following(i, carry):
+        to_tokens(i)
+        sum_core(i - 1)
+        return carry
+
+    lax.fori_loop(1, tp, following, 0)
+    sum_core(tp - 1)
     for i in range(tp):
-        to_tokens(i)
-        if i > 0:
-            sum_core(i - 1)
-    sum_core(tp - 1)
-    for i in range(tp - 1):
+        sent.append((None, to_partner(i)))
         for p in range(pieces):
-            z_out[i, part_of(p)] = sum_x(i, p).astype(b16)
-            n = pieces * i + p
-            view = pl.ds(p * piece, piece)
-            peer = {"tp": quarter(tp - 1 - i)}
-            send(z_out.at[i, view], z_in.at[i, view], rzs.at[n], rzr.at[n], peer)
+            sent.append((None, to_other_x(i, p)))
     for p in range(pieces):
+        pass_on(0, p)
+    for p in range(pieces):
+        for i in range(1, tp - 1):
+            pass_on(i, p)
+    for p in range(pieces):
+        view = pl.ds(p * piece, piece)
         result = sum_x(tp - 1, p)
-        for i in range(tp - 1):
-            n = pieces * i + p
-            peer = {"tp": lax.rem(t + tp - 1 - i, tp)}
-            got(z_in.at[i, pl.ds(p * piece, piece)], rzs.at[n], rzr.at[n], peer)
-            result = result + z_in[i, part_of(p)].astype(f32)
-        out[part_of(p), :] = result.astype(b16)
-    for cond, copy in some:
-
-        @pl.when(cond)
-        def _(copy=copy):
+        acc_g[part_of(p), 0:feat] = result
+        for cond, at in ((t > 0, t), (t < tp - 1, tp)):
+
+            @pl.when(cond)
+            def _(at=at):
+                got(z_in.at[at, view], rzs.at[0], rzr.at[pieces * at + p], above)
+                acc_g[part_of(p), 0:feat] += z_in[at, part_of(p)].astype(f32)
+
+        out[part_of(p), :] = acc_g[part_of(p), 0:feat].astype(b16)
+    for cond, copy in sent:
+        if cond is None:
             copy.wait_send()
-
-    for copy in sent:
-        copy.wait_send()
+        else:
+
+            @pl.when(cond)
+            def _(copy=copy):
+                copy.wait_send()
 
 
 def kernel_body(tokens, routing, route_gates, expert_gate, expert_up, expert_down):
@@ -350,21 +423,19 @@
     cap = 2 * tok // ep + tok // 16
     rows = up_to(ep * cap, 16)
     slots = up_to(rows, LANES)
-    ids = jnp.pad(routing.astype(jnp.float32).T, ((0, 0), (0, LANES - tok)), constant_values=-1.0)
-    weights = jnp.pad(route_gates.T, ((0, 4), (0, LANES - tok)))
-    meta = jnp.concatenate([ids, weights], axis=0)
     f32, b16 = jnp.float32, jnp.bfloat16
     dma = pltpu.SemaphoreType.DMA
     vmem = pl.BlockSpec(memory_space=pltpu.VMEM)
     hbm = pl.BlockSpec(memory_space=pl.ANY)
     return pl.pallas_call(
         functools.partial(layer_kernel, tp, ep, cap, rows),
-        out_shape=jax.ShapeDtypeStruct((tok, feat), b16),
-        in_specs=[vmem, vmem, hbm, hbm, hbm],
+        out_shape=pltpu.VMEM((tok, feat), b16),
+        in_specs=[hbm, vmem, vmem, hbm, hbm, hbm],
         out_specs=vmem,
         scratch_shapes=[
             pltpu.VMEM((tp, ep, LANES, feat), b16),
             pltpu.VMEM((ep, 8, LANES), f32),
+            pltpu.VMEM((8, LANES), f32),
             pltpu.VMEM((slots, ep * LANES), b16),
             pltpu.VMEM((ep * tok, slots), b16),
             pltpu.VMEM((slots, LANES), f32),
@@ -375,13 +446,13 @@
             pltpu.VMEM((rows, ff), f32),
             pltpu.VMEM((rows, feat), b16),
             pltpu.VMEM((rows, ff), b16),
-            pltpu.VMEM((slots, feat), b16),
             pltpu.VMEM((tp, ep, tok, feat), b16),
             pltpu.VMEM((tp, ep // 2, tok, feat), b16),
             pltpu.VMEM((tp, tok, feat), b16),
             pltpu.VMEM((tp, tok, feat), b16),
             pltpu.VMEM((tp, tok, feat), b16),
-            pltpu.VMEM((tp, tok, feat), b16),
+            pltpu.VMEM((tp + 1, tok, feat), b16),
+            dma((1,)),
             dma((3 * tp,)),
             dma((4 * tp,)), dma((2 * tp,)),
             dma((2 * tp,)), dma((2 * tp,)),
@@ -389,12 +460,12 @@
             dma((3,)), dma((3,)),
             dma((tp,)), dma((tp,)),
             dma((2 * tp,)), dma((2 * tp,)),
-            dma((2 * tp,)), dma((2 * tp,)),
+            dma((2 * tp,)), dma((2 * tp + 2,)),
         ],
         compiler_params=pltpu.CompilerParams(
             collective_id=0, has_side_effects=True, vmem_limit_bytes=60 * 1024 * 1024
         ),
-    )(tokens, meta, expert_gate, expert_up, expert_down)
+    )(tokens, routing.T, route_gates.T, expert_gate, expert_up, expert_down)
 
 
 def body(tokens, routing, route_gates, expert_gate, expert_up, expert_down):

time: 56.7 us -> 50.4 us (0.89)
  Pallas kernels: 52.9 us -> 49.6 us
  other arithmetic: 1.96 us -> 0 us
  local copies, waits for them, and re-layouts: 1.58 us -> 0.66 us
    pallas_call x1, Pallas kernels: 52.9 us -> 49.6 us  [kernel_body(): pl.pallas_call(functools.partial(layer_kernel, tp, ep, cap, rows), out_sh...]
    concatenate x1 -> x0, other arithmetic: 1.28 us -> none  [kernel_body(): meta = jnp.concatenate([ids, weights], axis=0)]
    unnamed x1, local copies, waits for them, and re-layouts: 1.58 us -> 0.66 us
    transpose x1 -> x0, other arithmetic: 0.68 us -> none  [kernel_body(): routing.astype(jnp.float32)]
where the time goes in v1:
time: 50.4 us; the launch traced here: 50.3 us
  Pallas kernels  49.6 us (98%)
  local copies, waits for them, and re-layouts  0.66 us (1%)
    pallas_call x1, Pallas kernels, kernel_body(): pl.pallas_call(functools.partial(layer_kernel, tp, ep, cap, rows), out_sh...  49.6 us

profile of v1, /device:TPU:0, one launch (start us, length us, event | category | flops | bytes accessed | tf_op | source)
XLA Modules:
  0.0 50.3 jit_solution(6776334850953053972)
XLA Ops:
  0.0 49.6 %shard_map.64 = bf16[96,768]{1,0:T(8,128)(2,1)S(1)} custom-call(bf16[96,768]{1,0:T(8,128)(2,1)} %tokens.1, s32[2,96]{1,0:T(2,128)} %bitcast.2, f32[2,96]{1,0:T(2,128)} %bitcast.3, bf16[1,3072,2048]{2,1,0:T(8,128)(2,1)} %gate_hbm.1, bf16[1,3072,2048]{2,1,0:T(8,128)(2,1)} %up_hbm.1, bf16[1,2048,3072]{2,1,0:T(8,128)(2,1)} %down_hbm.1), custom_call_target="tpu_custom_call" | custom-call | tf_op jit(solution)/shard_map/pallas_call | solution.py:430
  49.6 0.7 %copy.8 = bf16[96,768]{1,0:T(8,128)(2,1)} copy(bf16[96,768]{1,0:T(8,128)(2,1)S(1)} %shard_map.64) | data formatting | bytes 294912

commit v2 on v1

v2 whole, which is shorter than its diff:
```python
import functools

import jax
import jax.numpy as jnp
from jax import lax
from jax.experimental import pallas as pl
from jax.experimental.pallas import tpu as pltpu
from jax.sharding import PartitionSpec as P


def slot_tables(routing, route_gates, experts, capacity):
    count_rows = routing.shape[0]
    choices_n = routing.shape[1]
    flat_ids = routing.reshape(-1)
    onehot = (flat_ids[:, None] == jnp.arange(experts, dtype=jnp.int32)[None, :]).astype(jnp.int32)
    before = jnp.cumsum(onehot, axis=0) - onehot
    position = jnp.sum(before * onehot, axis=1)
    slot_index = flat_ids * capacity + position
    picked = (
        slot_index[:, None] == jnp.arange(experts * capacity, dtype=jnp.int32)[None, :]
    ).astype(jnp.float32)
    dispatch = picked.reshape(count_rows, choices_n, experts * capacity).sum(axis=1)
    combine = (
        (picked * route_gates.reshape(-1)[:, None])
        .reshape(count_rows, choices_n, experts * capacity)
        .sum(axis=1)
    )
    return (dispatch, combine)


def hidden_rows(everyone, expert_gate, expert_up, capacity):
    local_count = expert_gate.shape[0]
    total = everyone.shape[0]
    row_block = everyone.reshape(
        total // (local_count * capacity), local_count, capacity, everyone.shape[1]
    )
    gate_part = jnp.einsum(
        "tlcd,ldf->tlcf", row_block, expert_gate, preferred_element_type=jnp.float32
    )
    upward = jnp.einsum("tlcd,ldf->tlcf", row_block, expert_up, preferred_element_type=jnp.float32)
    return (jax.nn.silu(gate_part) * upward).astype(jnp.bfloat16)


def plain_body(tokens, routing, route_gates, expert_gate, expert_up, expert_down):
    local_count = expert_gate.shape[0]
    ep_count = lax.axis_size("ep")
    tp_count = lax.axis_size("tp")
    tok_count = tokens.shape[0]
    capacity = 2 * tok_count // ep_count + tok_count // 16
    experts = local_count * ep_count
    dispatch, combine = slot_tables(routing, route_gates, experts, capacity)
    dispatch_low = dispatch.astype(jnp.bfloat16)
    whole = lax.all_gather(tokens, "tp", axis=1, tiled=True)
    packed = jnp.einsum(
        "tc,td->cd", dispatch_low, whole, preferred_element_type=jnp.float32
    ).astype(jnp.bfloat16)
    everyone = lax.all_to_all(packed, "ep", split_axis=0, concat_axis=0, tiled=True)
    total_rows = everyone.shape[0]
    columns = everyone.shape[1]
    hidden = hidden_rows(everyone, expert_gate, expert_up, capacity)
    part = jnp.einsum("tlcf,lfd->dtlc", hidden, expert_down, preferred_element_type=jnp.float32)
    summed_t = lax.psum_scatter(
        part.reshape(columns // tp_count * lax.axis_size("tp"), total_rows),
        "tp",
        scatter_dimension=0,
        tiled=True,
    )
    summed = summed_t.T
    expert_out = summed.astype(jnp.bfloat16)
    returned = lax.all_to_all(expert_out, "ep", split_axis=0, concat_axis=0, tiled=True)
    mixed = jnp.dot(combine, returned.astype(jnp.float32), precision=lax.Precision.HIGHEST)
    return mixed.astype(jnp.bfloat16)


MESH = pl.DeviceIdType.MESH
LANES = 128
WIDE = 256


def up_to(value, step):
    return -(-value // step) * step


def row_spans(tok):
    units = tok // 16
    first = max(1, units // 6)
    second = (units - first + 1) // 2
    sizes = [16 * first, 16 * second, tok - 16 * (first + second)]
    return [(sum(sizes[:k]), sizes[k]) for k in range(3)]


def rcopy(src, dst, send, recv, device):
    return pltpu.make_async_remote_copy(
        src_ref=src, dst_ref=dst, send_sem=send, recv_sem=recv, device_id=device, device_id_type=MESH
    )


def layer_kernel(
    tp, ep, cap, rows, tokens, routing, gates, gate_hbm, up_hbm, down_hbm, out,
    x, m, m_own, pick, place, scale, wg, wu, wd, acc_g, acc_u, packed, hidden,
    c, c_in, x_out, x_in, y_out, y_in, f_out, f_in, z_out, z_in,
    t_sem, w_sem, zs, zr, xs, xr, cs, cr, ms, mr,
    rcs, rcr, rxs, rxr, rys, ryr, rfs, rfr, rzs, rzr,
):
    t = lax.axis_index("tp")
    e = lax.axis_index("ep")
    half = ep // 2
    core = lax.rem(e, 2)
    column = e // 2
    e_core = e + 1 - 2 * core
    e_x = lax.rem(e + half, ep)
    e_xc = lax.rem(e_core + half, ep)
    tok, feat = tokens.shape
    ff = wg.shape[2]
    nt = feat // WIDE
    f32, b16 = jnp.float32, jnp.bfloat16
    to_x, to_core = {"ep": e_x}, {"ep": e_core}
    above, below = {"tp": lax.rem(t + 1, tp)}, {"tp": lax.rem(t + tp - 1, tp)}

    barrier = pltpu.get_barrier_semaphore()

    @pl.when(t < tp - 1)
    def _():
        pl.semaphore_signal(barrier, inc=1, device_id=above, device_id_type=MESH)

    @pl.when(t > 0)
    def _():
        pl.semaphore_signal(barrier, inc=1, device_id=below, device_id_type=MESH)

    pl.semaphore_signal(barrier, inc=1, device_id=to_x, device_id_type=MESH)
    pl.semaphore_signal(barrier, inc=1, device_id=to_core, device_id_type=MESH)

    own_load = pltpu.make_async_copy(tokens, x.at[t, e, pl.ds(0, tok), :], t_sem.at[0])
    own_load.start()

    def select(values):
        found = jnp.int32(values[0])
        for k in range(1, tp):
            found = jnp.where(t == k, jnp.int32(values[k]), found)
        return found

    def near(k):
        return sorted(range(tp), key=lambda q: (abs(q - k), q))

    def far(k):
        return sorted(range(tp), key=lambda q: (-abs(q - k), abs(2 * q - tp + 1), q))

    arrivals = [select([near(k)[i] for k in range(tp)]) for i in range(tp)]
    leaving = [select([far(k)[i] for k in range(tp)]) for i in range(tp)]
    spans = row_spans(tok)
    pieces = len(spans)
    bulk = range(1, pieces)

    loads = []
    for d in range(tp):
        q = arrivals[d]
        for k, (src, dst) in enumerate(((gate_hbm, wg), (up_hbm, wu))):
            r = pl.ds(pl.multiple_of(q * feat, feat), feat)
            loads.append(pltpu.make_async_copy(src.at[0, r, :], dst.at[q], w_sem.at[k * tp + d]))
    down_loads = []
    for i in range(tp):
        q = leaving[i]
        r = pl.ds(pl.multiple_of(q * feat, feat), feat)
        down_loads.append(pltpu.make_async_copy(down_hbm.at[0, :, r], wd.at[q], w_sem.at[2 * tp + i]))
    pad = x.shape[2] - tok
    for q in range(tp):
        for b in range(ep):
            x[q, b, tok:, :] = jnp.zeros((pad, feat), b16)
    m_own[...] = jnp.full(m_own.shape, -1.0, f32)
    m_own[0:2, 0:tok] = routing[...].astype(f32)
    m_own[2:4, 0:tok] = gates[...]
    m[e] = m_own[...]

    edge = (t == 0) | (t == tp - 1)

    @pl.when(t == 0)
    def _():
        y_in[0:tp] = jnp.zeros((tp, *y_in.shape[1:]), b16)
        z_in[0:tp * nt] = jnp.zeros((tp * nt, *z_in.shape[1:]), b16)

    @pl.when(t == tp - 1)
    def _():
        y_in[0:tp - 1] = jnp.zeros((tp - 1, *y_in.shape[1:]), b16)
        y_in[tp] = jnp.zeros(y_in.shape[1:], b16)
        z_in[0:(tp - 1) * nt] = jnp.zeros(((tp - 1) * nt, *z_in.shape[1:]), b16)
        z_in[tp * nt:] = jnp.zeros((nt, *z_in.shape[1:]), b16)

    own_load.wait()
    for load in loads + down_loads:
        load.start()
    pl.semaphore_wait(barrier, 2 + jnp.where(t > 0, 1, 0) + jnp.where(t < tp - 1, 1, 0))

    def send(src, dst, s, r, device):
        rcopy(src, dst, s, r, device).start()

    def block(q, b, p):
        return x.at[q, b, pl.ds(*spans[p]), :]

    def send_if(cond, src, dst, s, r, device):
        @pl.when(cond)
        def _():
            send(src, dst, s, r, device)

    def at(side, q, p):
        return (side * tp + q) * pieces + p

    def up_down(side, q, p, up, cond):
        one = block(q, (e, e_x)[side], p)
        n = at(side, q, p)
        send_if(cond, one, one, zs.at[at(2 * up + side, q, p)], zr.at[n], above if up else below)

    send(m_own, m.at[e], ms.at[0], mr.at[0], to_x)
    send(m_own, m.at[e], ms.at[1], mr.at[1], to_core)
    for p in (*bulk, 0):
        own = block(t, e, p)
        n = at(0, t, p)
        send(own, own, xs.at[n], xr.at[n], to_x)
        up_down(0, t, p, 1, t < tp - 1)
        up_down(0, t, p, 0, t > 0)
        send(own, own, cs.at[n], cr.at[n], to_core)

    def got(dst, s, r, device):
        rcopy(dst, dst, s, r, device).wait_recv()

    def take_z(d, ps, side=0):
        for p in ps:
            for up in (1, 0):
                q = t - d if up else t + d
                here = q >= 0 if up else q < tp
                onward = here & (t < tp - 1 if up else t > 0)
                q = jnp.clip(q, 0, tp - 1)
                one = block(q, (e, e_x)[side], p)
                n = at(side, q, p)

                @pl.when(here)
                def _(one=one, n=n, p=p):
                    got(one, zs.at[0], zr.at[n], above)
                    if p > 0:
                        send(one, one, xs.at[n], xr.at[n], to_x)
                    send(one, one, cs.at[n], cr.at[n], to_core)

                up_down(side, q, p, up, onward)

    def take_x(i, ps):
        q = arrivals[i]
        for p in ps:
            one = block(q, e_x, p)
            got(one, xs.at[0], xr.at[at(0, q, p)], to_x)
            if p == 0:
                up_down(1, q, p, 1, t < tp - 1)
                up_down(1, q, p, 0, t > 0)
            n = at(1, q, p)
            send(one, one, cs.at[n], cr.at[n], to_core)

    def take_core(i):
        q = arrivals[i]
        for p in range(pieces):
            got(block(q, e_core, p), cs.at[0], cr.at[at(0, q, p)], to_core)
            got(block(q, e_xc, p), cs.at[0], cr.at[at(1, q, p)], to_core)

    def take_meta():
        got(m.at[e_core], ms.at[1], mr.at[1], to_core)
        got(m.at[e_xc], ms.at[2], mr.at[2], to_core)

    got(m.at[e_x], ms.at[0], mr.at[0], to_x)
    send(m.at[e_x], m.at[e_x], ms.at[2], mr.at[2], to_core)
    take_z(1, [1])
    take_meta()

    slots = pick.shape[0]
    mine = e.astype(f32)
    earlier = (
        lax.broadcasted_iota(jnp.int32, (LANES, LANES), 0)
        < lax.broadcasted_iota(jnp.int32, (LANES, LANES), 1)
    ).astype(b16)
    slot = lax.broadcasted_iota(jnp.int32, (slots, LANES), 0).astype(f32)
    total = jnp.zeros((slots, 1), f32)
    for b in range(ep):
        first, second = m[b, 0:1, :] == mine, m[b, 1:2, :] == mine
        named = jnp.where(first, 1.0, 0.0) + jnp.where(second, 1.0, 0.0)
        weight = jnp.where(first, m[b, 2:3, :], 0.0) + jnp.where(second, m[b, 3:4, :], 0.0)
        spread = jnp.broadcast_to(named, (16, LANES)).astype(b16)
        position = jnp.dot(spread, earlier, preferred_element_type=f32)[0:1, :]
        where_to = jnp.where(named > 0.5, position + float(b * cap), -1.0)
        chosen = jnp.where(slot == where_to, 1.0, 0.0)
        total = total + jnp.sum(chosen * weight, axis=1, keepdims=True)
        pick[:, b * LANES:(b + 1) * LANES] = chosen.astype(b16)
        base = ((b % 2) * half + b // 2) * tok
        place[base:base + tok, :] = chosen.T[0:tok, :].astype(b16)
    scale[...] = jnp.broadcast_to(total, scale.shape)

    step = ff // 2
    acc_g[...] = jnp.zeros(acc_g.shape, f32)
    acc_u[...] = jnp.zeros(acc_u.shape, f32)

    def chosen_at(values, i):
        found = values[0]
        for k in range(1, tp):
            found = jnp.where(i == k, values[k], found)
        return found

    def gather(d):
        q = chosen_at(arrivals, d)
        r = pl.ds(pl.multiple_of(q * feat, feat), feat)
        for k, (src, dst) in enumerate(((gate_hbm, wg), (up_hbm, wu))):
            pltpu.make_async_copy(src.at[0, r, :], dst.at[q], w_sem.at[k * tp + d]).wait()
        everyone = x[q].reshape(ep * x.shape[2], feat)
        packed[...] = jnp.dot(pick[0:rows, :], everyone, preferred_element_type=f32).astype(b16)

    def project(d, cols, last):
        q = chosen_at(arrivals, d)
        g = jnp.dot(packed[...], wg[q, :, cols], preferred_element_type=f32) + acc_g[:, cols]
        u = jnp.dot(packed[...], wu[q, :, cols], preferred_element_type=f32) + acc_u[:, cols]
        if last:
            h = g / (1.0 + jnp.exp(-g)) * u * scale[0:rows, 0:1]
            hidden[:, cols] = h.astype(b16)
        else:
            acc_g[:, cols] = g
            acc_u[:, cols] = u

    take_z(1, bulk[1:])
    take_x(0, bulk)
    take_z(1, [0])
    take_x(0, [0])
    take_core(0)

    def between(n):
        d = (n + 1) // 2
        if n % 2 == 0:
            take_core(d)
            return
        take_z(d + 1, bulk)
        take_x(d, bulk)
        take_z(d + 1, [0])
        take_z(d, [0], 1)

    def half_step(n, carry):
        for k in range(1, 2 * tp - 2):

            @pl.when(n == k)
            def _(k=k):
                between(k)

        @pl.when(n % 2 == 0)
        def _():
            gather(n // 2)

        project(n // 2, pl.ds(pl.multiple_of((n % 2) * step, step), step), False)
        return carry

    lax.fori_loop(0, 2 * tp - 2, half_step, 0)
    take_core(tp - 1)
    gather(tp - 1)
    for j in range(4):
        project(tp - 1, slice(j * ff // 4, (j + 1) * ff // 4), True)

    tail = jnp.zeros((slots - rows, WIDE), b16)
    low, high = slice(0, LANES), slice(LANES, WIDE)

    def to_partner(k):
        away = pl.ds((1 - core) * half, half)
        return rcopy(c.at[k, away], c_in.at[k], rcs.at[k], rcr.at[k], to_core)

    def to_tokens(i, j):
        cols = slice(j * WIDE, (j + 1) * WIDE)
        q = chosen_at(leaving, i)
        part = jnp.dot(hidden[...], wd[q, :, cols], preferred_element_type=f32).astype(b16)
        part = jnp.concatenate([part, tail], axis=0) if slots > rows else part
        back = jnp.dot(place[...], part, preferred_element_type=f32).astype(b16)
        c[i * nt + j] = back.reshape(ep, tok, WIDE)

    def both_cores(k, col, cols=slice(None)):
        return c[k, core * half + col, :, cols].astype(f32) + c_in[k, col, :, cols].astype(f32)

    def in_x(ref, k, first):
        return ref.at[k, :, pl.ds(LANES, LANES)] if first else ref.at[k]

    def to_other_x(k, first):
        return rcopy(in_x(x_out, k, first), in_x(x_in, k, first), rxs.at[k], rxr.at[k], to_x)

    def sum_core(i, j):
        k = i * nt + j
        got(c_in.at[k], rcs.at[0], rcr.at[k], to_core)
        x_out[k] = both_cores(k, 1 - column).astype(b16)

        to_other_x(k, j == 0).start()

    def along(i):
        q = chosen_at(leaving, i)
        right = q > t
        slot_to = jnp.where(~right & (q == t - 1), tp, q)
        return q, slot_to, {"tp": jnp.where(right, lax.rem(t + 1, tp), lax.rem(t + tp - 1, tp))}

    def low_copy(i):
        q, slot_to, peer = along(i)
        return rcopy(y_out.at[i], y_in.at[slot_to], rys.at[i], ryr.at[slot_to], peer)

    def pass_low(i, cond):
        q = chosen_at(leaving, i)

        @pl.when(cond)
        def _():
            @pl.when(~edge)
            def _():
                got(y_in.at[q], rys.at[0], ryr.at[q], above)

            for col in range(half):
                y_out[i, col] = (both_cores(i * nt, col, low) + y_in[q, col].astype(f32)).astype(b16)
            low_copy(i).start()

    def to_own(one):
        @pl.when(t > 0)
        def _():
            one(t)

        @pl.when(t < tp - 1)
        def _():
            one(jnp.int32(tp))

    def to_own_low(at_slot):
        got(y_in.at[at_slot], rys.at[0], ryr.at[at_slot], above)

    def to_own_bulk(j):
        def one(at_slot):
            k = at_slot * nt + j
            got(in_x(z_in, k, j == 0), rzs.at[0], rzr.at[k], above)

        to_own(one)

    def low_sum(col):
        arrived = y_in[t, col].astype(f32) + y_in[tp, col].astype(f32)
        return both_cores((tp - 1) * nt, col, low) + arrived

    def finish_low():
        to_own(to_own_low)
        f_out[...] = low_sum(1 - column).astype(b16)
        send(f_out, f_in, rfs.at[0], rfr.at[0], to_x)

    def sum_x(i, j):
        k, cols = i * nt + j, high if j == 0 else slice(None)
        got(in_x(x_in, k, j == 0), rxs.at[0], rxr.at[k], to_x)
        return both_cores(k, column, cols) + x_in[k, :, cols].astype(f32)

    def bulk_copy(i, j):
        q, slot_to, peer = along(i)
        k, k_to = i * nt + j, slot_to * nt + j
        first = j == 0
        return rcopy(in_x(z_out, k, first), in_x(z_in, k_to, first), rzs.at[k], rzr.at[k_to], peer)

    def pass_on(i, j):
        k, k_in, cols = i * nt + j, chosen_at(leaving, i) * nt + j, high if j == 0 else slice(None)
        value = sum_x(i, j)

        @pl.when(~edge)
        def _():
            got(in_x(z_in, k_in, j == 0), rzs.at[0], rzr.at[k_in], above)

        z_out[k, :, cols] = (value + z_in[k_in, :, cols].astype(f32)).astype(b16)
        bulk_copy(i, j).start()

    def leave(i):
        r = pl.ds(pl.multiple_of(chosen_at(leaving, i) * feat, feat), feat)
        q = chosen_at(leaving, i)
        pltpu.make_async_copy(down_hbm.at[0, :, r], wd.at[q], w_sem.at[2 * tp + i]).wait()

    leave(0)
    for j in range(nt):
        to_tokens(0, j)
    for j in range(nt):
        to_partner(j).start()

    def following(i, carry):
        leave(i)
        for j in range(nt):
            to_tokens(i, j)
        for j in range(nt):
            to_partner(i * nt + j).start()
        for j in range(nt):
            sum_core(i - 1, j)
        pass_low(i - 1, edge)
        return carry

    lax.fori_loop(1, tp, following, 0)

    @pl.when(edge)
    def _():
        for j in range(nt - 1):
            pass_on(0, j)

    for j in range(nt):
        sum_core(tp - 1, j)
    pass_low(0, ~edge)
    for i in range(1, tp - 2):
        pass_low(i, ~edge)

    @pl.when(~edge)
    def _():
        for j in range(nt - 1):
            pass_on(0, j)

    pass_low(tp - 2, ~edge)
    pass_on(0, nt - 1)

    @pl.when(edge)
    def _():
        def by_quarter(i, carry):
            for j in range(nt):
                pass_on(i, j)
            return carry

        lax.fori_loop(1, tp - 1, by_quarter, 0)

    @pl.when(~edge)
    def _():
        for j in range(nt):

            def by_piece(i, carry, j=j):
                pass_on(i, j)
                return carry

            lax.fori_loop(1, tp - 1, by_piece, 0)

    finish_low()
    for j in range(nt):
        cols = high if j == 0 else slice(None)
        start = LANES if j == 0 else j * WIDE
        result = sum_x(tp - 1, j)
        to_own_bulk(j)
        result = result + z_in[t * nt + j, :, cols].astype(f32) + z_in[tp * nt + j, :, cols].astype(f32)
        out[:, start:(j + 1) * WIDE] = result.astype(b16)
    got(f_in, rfs.at[0], rfr.at[0], to_x)
    out[:, low] = (low_sum(column) + f_in[...].astype(f32)).astype(b16)

    def left(src, s):
        rcopy(src, src, s, xr.at[0], to_x).wait_send()

    for n in range(3):
        left(m_own, ms.at[n])
    left(f_out, rfs.at[0])
    left(block(t, e, 0), xs.at[at(0, t, 0)])
    for q in range(tp):
        for p in range(pieces):
            one = block(q, e, p)
            left(one, cs.at[at(0, q, p)])
            left(one, cs.at[at(1, q, p)])
            if p > 0:
                left(one, xs.at[at(0, q, p)])
        for up in (1, 0):

            @pl.when((q <= t) & (t < tp - 1) if up else (q >= t) & (t > 0))
            def _(q=q, up=up):
                for p in range(pieces):
                    left(block(q, e, p), zs.at[at(2 * up, q, p)])
                left(block(q, e_x, 0), zs.at[at(2 * up + 1, q, 0)])

    for i in range(tp):
        for j in range(nt):
            to_partner(i * nt + j).wait_send()
            to_other_x(i * nt + j, j == 0).wait_send()
            if i < tp - 1:
                bulk_copy(i, j).wait_send()
        if i < tp - 1:
            low_copy(i).wait_send()


def kernel_body(tokens, routing, route_gates, expert_gate, expert_up, expert_down):
    ep, tp = lax.axis_size("ep"), lax.axis_size("tp")
    tok, feat = tokens.shape
    ff = expert_gate.shape[2]
    cap = 2 * tok // ep + tok // 16
    rows = up_to(ep * cap, 16)
    slots = up_to(rows, LANES)
    nt, pieces = feat // WIDE, len(row_spans(tok))
    f32, b16 = jnp.float32, jnp.bfloat16
    dma = pltpu.SemaphoreType.DMA
    vmem = pl.BlockSpec(memory_space=pltpu.VMEM)
    hbm = pl.BlockSpec(memory_space=pl.ANY)
    return pl.pallas_call(
        functools.partial(layer_kernel, tp, ep, cap, rows),
        out_shape=pltpu.VMEM((tok, feat), b16),
        in_specs=[hbm, vmem, vmem, hbm, hbm, hbm],
        out_specs=vmem,
        scratch_shapes=[
            pltpu.VMEM((tp, ep, LANES, feat), b16),
            pltpu.VMEM((ep, 8, LANES), f32),
            pltpu.VMEM((8, LANES), f32),
            pltpu.VMEM((slots, ep * LANES), b16),
            pltpu.VMEM((ep * tok, slots), b16),
            pltpu.VMEM((slots, LANES), f32),
            pltpu.VMEM((tp, feat, ff), b16),
            pltpu.VMEM((tp, feat, ff), b16),
            pltpu.VMEM((tp, ff, feat), b16),
            pltpu.VMEM((rows, ff), f32),
            pltpu.VMEM((rows, ff), f32),
            pltpu.VMEM((rows, feat), b16),
            pltpu.VMEM((rows, ff), b16),
            pltpu.VMEM((tp * nt, ep, tok, WIDE), b16),
            pltpu.VMEM((tp * nt, ep // 2, tok, WIDE), b16),
            pltpu.VMEM((tp * nt, tok, WIDE), b16),
            pltpu.VMEM((tp * nt, tok, WIDE), b16),
            pltpu.VMEM((tp, ep // 2, tok, LANES), b16),
            pltpu.VMEM((tp + 1, ep // 2, tok, LANES), b16),
            pltpu.VMEM((tok, LANES), b16),
            pltpu.VMEM((tok, LANES), b16),
            pltpu.VMEM((tp * nt, tok, WIDE), b16),
            pltpu.VMEM(((tp + 1) * nt, tok, WIDE), b16),
            dma((1,)),
            dma((3 * tp,)),
            dma((4 * tp * pieces,)), dma((2 * tp * pieces,)),
            dma((tp * pieces,)), dma((tp * pieces,)),
            dma((2 * tp * pieces,)), dma((2 * tp * pieces,)),
            dma((3,)), dma((3,)),
            dma((tp * nt,)), dma((tp * nt,)),
            dma((tp * nt,)), dma((tp * nt,)),
            dma((tp,)), dma((tp + 1,)),
            dma((1,)), dma((1,)),
            dma((tp * nt,)), dma(((tp + 1) * nt,)),
        ],
        compiler_params=pltpu.CompilerParams(
            collective_id=0, has_side_effects=True, vmem_limit_bytes=60 * 1024 * 1024
        ),
    )(tokens, routing.T, route_gates.T, expert_gate, expert_up, expert_down)


def body(tokens, routing, route_gates, expert_gate, expert_up, expert_down):
    ep, tp = lax.axis_size("ep"), lax.axis_size("tp")
    tok, feat = tokens.shape
    ff = expert_gate.shape[2]
    fits = ep == 4 and 2 < tp < 5 and expert_gate.shape[0] == 1 and 48 <= tok <= LANES and tok % 16 == 0
    fits = fits and feat % WIDE == 0 and ff % 512 == 0 and 3 * tp * feat * ff * 2 <= 40 << 20
    run = kernel_body if fits else plain_body
    return run(tokens, routing, route_gates, expert_gate, expert_up, expert_down)


def solution(mesh):
    return jax.shard_map(
        body,
        mesh=mesh,
        in_specs=(
            P(("rep", "ep"), "tp"),
            P(("rep", "ep"), None),
            P(("rep", "ep"), None),
            P("ep", None, "tp"),
            P("ep", None, "tp"),
            P("ep", "tp", None),
        ),
        out_specs=P(("rep", "ep"), "tp"),
        check_vma=False,
    )
```

time: 50.4 us -> 46 us (0.913)
  Pallas kernels: 49.6 us -> 45.1 us
    pallas_call x1, Pallas kernels: 49.6 us -> 45.1 us  [kernel_body(): pl.pallas_call(functools.partial(layer_kernel, tp, ep, cap, rows), out_sh...]
where the time goes in v2:
time: 46 us; the launch traced here: 45.8 us
  Pallas kernels  45.1 us (98%)
  local copies, waits for them, and re-layouts  0.66 us (1%)
    pallas_call x1, Pallas kernels, kernel_body(): pl.pallas_call(functools.partial(layer_kernel, tp, ep, cap, rows), out_sh...  45.1 us

profile of v2, /device:TPU:0, one launch (start us, length us, event | category | flops | bytes accessed | tf_op | source)
XLA Modules:
  0.0 45.8 jit_solution(1778070917265316967)
XLA Ops:
  0.0 45.1 %shard_map.64 = bf16[96,768]{1,0:T(8,128)(2,1)S(1)} custom-call(bf16[96,768]{1,0:T(8,128)(2,1)} %tokens.1, s32[2,96]{1,0:T(2,128)} %bitcast.2, f32[2,96]{1,0:T(2,128)} %bitcast.3, bf16[1,3072,2048]{2,1,0:T(8,128)(2,1)} %gate_hbm.1, bf16[1,3072,2048]{2,1,0:T(8,128)(2,1)} %up_hbm.1, bf16[1,2048,3072]{2,1,0:T(8,128)(2,1)} %down_hbm.1), custom_call_target="tpu_custom_call" | custom-call | tf_op jit(solution)/shard_map/pallas_call | solution.py:578
  45.2 0.7 %copy.8 = bf16[96,768]{1,0:T(8,128)(2,1)} copy(bf16[96,768]{1,0:T(8,128)(2,1)S(1)} %shard_map.64) | data formatting | bytes 294912
